TPU v7x, 256 devices: a whole 4x4x8 slice. The times are simulated.
256 devices in a mesh: vox: 128 (over x, z, y), sub: 2 (over core).
Axes of the slice: x: 4, y: 4, z: 8, core: 2. Of those that a mesh axis runs over, the one named last changes fastest.
Arguments:
- movie: bfloat16 [262144, 4096], P(('vox', 'sub')), may hold values from -120 to 120
- test_matrix: bfloat16 [4096, 256], replicated, may hold values from -0.09375 to 0.09375
Outputs:
- basis: float32 [262144, 256], P(('vox', 'sub'))
- r_factor: float32 [256, 256], replicated
- projected: float32 [256, 4096], P(None, ('vox', 'sub'))
All inputs are finite; a program needn't handle non-finite values.
Results may differ from a plain program's by a relative error of at most 0.00063.
Values sent between devices are 32-bit elements; how exact they have to be, the bound alone decides.
A program may use at most 128 MiB of HBM per device.

v0:
```python
import jax
import jax.numpy as jnp
from jax import lax
from jax.sharding import PartitionSpec as P


def square_sum(matrix):
    return jnp.dot(matrix.T, matrix, precision=lax.Precision.HIGHEST)


def local(movie, test_matrix):
    sketch = jnp.dot(movie, test_matrix, preferred_element_type=jnp.float32)
    devices_all = lax.axis_size(("vox", "sub"))
    sketch_b = sketch.astype(jnp.bfloat16)
    partial_sum = lax.dot_general(
        sketch_b, movie, (((0,), (0,)), ((), ())), preferred_element_type=jnp.float32
    )
    columns = movie.shape[1] // devices_all
    total = lax.psum(partial_sum, ("vox", "sub"))
    mine = lax.dynamic_slice_in_dim(total, lax.axis_index(("vox", "sub")) * columns, columns, 1)
    gram = lax.psum(square_sum(sketch), ("vox", "sub"))
    lower = jnp.linalg.cholesky(gram)
    width = sketch.shape[1]
    identity = jnp.eye(width, dtype=jnp.float32)
    inverse = lax.linalg.triangular_solve(lower, identity, left_side=True, lower=True)
    scale = jnp.sqrt(jnp.float32(sketch.shape[0] * devices_all))
    basis = jnp.dot(sketch, inverse.T, precision=lax.Precision.HIGHEST) * scale
    projected = jnp.dot(inverse, mine, precision=lax.Precision.HIGHEST)
    return (basis, lower.T / scale, projected)


def solution(mesh):
    placed = (P(("vox", "sub"), None), P())
    return jax.shard_map(
        local,
        mesh=mesh,
        in_specs=placed,
        out_specs=(P(("vox", "sub"), None), P(), P(None, ("vox", "sub"))),
        check_vma=False,
    )
```

profile of v0, /device:TPU:2, one launch (start us, length us, event | category | flops | bytes accessed | tf_op | source)
XLA Modules:
  0.0 380.6 jit_solution(14960276804258986143)
XLA Ops:
  7.2 0.0 copy-start
  7.2 0.0 all-reduce.4.cloned.1.call-start
  7.2 1.5 copy-done
  8.8 0.0 copy-start.1
  8.8 5.9 %fusion.17 = f32[1024,256]{1,0:T(8,128)S(1)} fusion(bf16[1024,4096]{1,0:T(8,128)(2,1)} %param.2, bf16[4096,256]{1,0:T(8,128)(2,1)S(1)} %copy-done), kind=kOutput, calls=%fused_computation.40 | convolution fusion | flops 2147483648 | bytes 11534336 | tf_op jit(solution)/shard_map/dot_general | solution.py:12
  14.6 0.0 copy-done.1
  14.6 4.3 %fusion = f32[256,4096]{1,0:T(8,128)} fusion(bf16[1024,4096]{1,0:T(8,128)(2,1)S(1)} %copy-done.1, f32[1024,256]{1,0:T(8,128)S(1)} %fusion.17), kind=kOutput, calls=%fused_computation.5 | convolution fusion | flops 2147745792 | bytes 13631488 | tf_op jit(solution)/shard_map/dot_general | solution.py:15
  19.0 2.5 fusion.18
  21.5 0.0 all-reduce.4.cloned.1.call-update
  21.6 0.6 iota_compare_fusion
  22.2 274.1 %all-reduce.4.cloned.1.call-done = (f32[256,256]{0,1:T(8,128)}, f32[256,4096]{1,0:T(8,128)}) async-done(((f32[256,256]{0,1:T(8,128)}, f32[256,4096]{1,0:T(8,128)}), (f32[256,256]{0,1:T(8,128)}, f32[256,4096]{1,0:T(8,128)})) %all-reduce.4.cloned.1.call-update) | async-done | bytes 4456464 | tf_op jit(solution)/shard_map/psum | solution.py:21
  296.3 1.1 copy.6
  297.3 1.0 fusion.2
  298.3 0.0 copy-start.3
  298.3 0.7 copy-done.3
  299.0 11.7 %cholesky.50 = f32[128,128]{1,0:T(8,128)S(1)} custom-call(f32[128,128]{1,0:T(8,128)S(1)} %cholesky.118), custom_call_target="Cholesky" | custom-call | tf_op jit(solution)/shard_map/jit(cholesky)/cholesky | solution.py:22
  310.8 9.8 %custom-call.14 = f32[1,128,128]{1,2,0:T(8,128)S(1)} custom-call(f32[1,128,128]{2,1,0:T(8,128)S(1)} %get-tuple-element.31), custom_call_target="InvertDiagBlocksLowerTriangular" | custom-call | tf_op jit(solution)/shard_map/jit(cholesky)/cholesky | solution.py:22
  320.6 0.2 cholesky.113
  320.8 1.0 constant_dynamic-update-slice_fusion
  321.9 1.1 convolution_subtract_fusion.1
  323.0 11.7 %cholesky.105 = f32[128,128]{1,0:T(8,128)S(1)} custom-call(f32[128,128]{1,0:T(8,128)S(1)} %convolution_subtract_fusion.1), custom_call_target="Cholesky" | custom-call | tf_op jit(solution)/shard_map/jit(cholesky)/cholesky | solution.py:22
  334.7 0.0 copy-start.2
  334.7 0.7 compare_reduce_fusion
  336.7 0.0 copy-done.2
  336.7 1.7 multiply_bitcast_fusion
  338.4 0.1 triangular_solve.63
  338.5 5.2 %while.1 = (s32[]{:T(128)}, f32[256,256]{1,0:T(8,128)S(1)}, s32[2,2]{1,0:T(2,128)S(1)}, f32[2,128,128]{2,1,0:T(8,128)}, s32[]{:T(128)}) while((s32[]{:T(128)}, f32[256,256]{1,0:T(8,128)S(1)}, s32[2,2]{1,0:T(2,128)S(1)}, f32[2,128,128]{2,1,0:T(8,128)}, s32[]{:T(128)}) %tuple.29), condition=%wide.while_cond, body=%wide.while_body.sunk | while | flops 2 | bytes 132705 | solution.py:25
  338.5 0.6 fusion.30
  339.1 2.0 bitcast_dynamic-update-slice_fusion.2
  341.1 0.6 fusion.30
  341.7 2.0 bitcast_dynamic-update-slice_fusion.2
  343.7 21.1 %custom-call.15 = f32[2,128,128]{1,2,0:T(8,128)} custom-call(f32[2,128,128]{2,1,0:T(8,128)} %get-tuple-element.10), custom_call_target="InvertDiagBlocksLowerTriangular" | custom-call | tf_op jit(solution)/shard_map/triangular_solve | solution.py:25
  364.8 1.1 fusion.6
  365.9 1.0 convolution_subtract_fusion
  366.9 1.2 fusion.9
  368.1 2.0 convolution_multiply_fusion
  370.1 1.8 copy.7
  371.8 1.9 fusion.4
  (7 shorter events, 0.1 us)
Async XLA Ops:
  7.2 1.6 copy-start
  7.2 289.1 %all-reduce.4.cloned.1.call-start = ((), (), s32[]{:S(2)}) async-start(), calls=%async_computation | async-start | bytes 8912896 | tf_op jit(solution)/shard_map/psum | solution.py:21
  8.8 5.9 %copy-start.1 = (bf16[1024,4096]{1,0:T(8,128)(2,1)S(1)}, bf16[1024,4096]{1,0:T(8,128)(2,1)}, u32[]{:S(2)}) copy-start(bf16[1024,4096]{1,0:T(8,128)(2,1)} %param.2) | copy-start | bytes 25165828
  298.3 0.7 copy-start.3
  334.7 2.0 copy-start.2
Sparse Core Ops, SparseCore 0:
  21.7 274.5 all-reduce.3
where the time goes:
time: 381 us
  waiting for transfers between devices  274 us (72%)
  other arithmetic  58.5 us (15%)
  matrix products  22.1 us (6%)
  between operations  15.4 us (4%)
  local copies, waits for them, and re-layouts  10.6 us (3%)
    psum x1, waiting for transfers between devices, local(): gram = lax.psum(square_sum(sketch), ('vox', 'sub'))  274 us
    another operation x6, other arithmetic, local(): lower = jnp.linalg.cholesky(gram)  34 us
    another operation x2, other arithmetic, local(): lax.linalg.triangular_solve(lower, identity, left_side=True, lower=True)  21.1 us
  transfers between devices with their start and end apart: 1, of which 1 were waited for; matrix products, arithmetic and copies ran while one was open for 0% of the time, Pallas kernels for 0%

commit v1 on v0

--- a/solution.py
+++ b/solution.py
@@ -2,6 +2,7 @@
 import jax.numpy as jnp
 from jax import lax
 from jax.sharding import PartitionSpec as P
+from jax.lax import psum
 
 
 def square_sum(matrix):
@@ -18,7 +19,9 @@
     columns = movie.shape[1] // devices_all
     total = lax.psum(partial_sum, ("vox", "sub"))
     mine = lax.dynamic_slice_in_dim(total, lax.axis_index(("vox", "sub")) * columns, columns, 1)
-    gram = lax.psum(square_sum(sketch), ("vox", "sub"))
+    gram = square_sum(sketch)
+    for c in ("sub", "vox"):
+        gram = psum(gram, c)
     lower = jnp.linalg.cholesky(gram)
     width = sketch.shape[1]
     identity = jnp.eye(width, dtype=jnp.float32)

time: 381 us -> 555 us (1.46)
  waiting for transfers between devices: 274 us -> 444 us
    psum x1 -> x3, waiting for transfers between devices: 274 us -> 444 us  [the longest x2 246 us: local(): gram = psum(gram, c)]
  transfers between devices with their start and end apart: 1 -> 3, of which waited for: 1 -> 3; matrix products, arithmetic and copies ran while one was open for 0% -> 15% of each run, Pallas kernels for 0% -> 0%
where the time goes in v1:
time: 555 us; the launch traced here: 554 us
  waiting for transfers between devices  444 us (80%)
  other arithmetic  58.5 us (11%)
  matrix products  25.3 us (5%)
  between operations  15.1 us (3%)
  local copies, waits for them, and re-layouts  10.2 us (2%)
    psum x2, waiting for transfers between devices, local(): gram = psum(gram, c)  246 us
    psum x1, waiting for transfers between devices, local(): total = lax.psum(partial_sum, ('vox', 'sub'))  199 us
    another operation x6, other arithmetic, local(): lower = jnp.linalg.cholesky(gram)  34.1 us
    another operation x2, other arithmetic, local(): lax.linalg.triangular_solve(lower, identity, left_side=True, lower=True)  21.1 us
  transfers between devices with their start and end apart: 3, of which 3 were waited for; matrix products, arithmetic and copies ran while one was open for 15% of the time, Pallas kernels for 0%

profile of v1, /device:TPU:2, one launch (start us, length us, event | category | flops | bytes accessed | tf_op | source)
XLA Modules:
  0.0 553.9 jit_solution(2074768162319565386)
XLA Ops:
  7.2 0.0 copy-start
  7.2 0.0 all-reduce.5.cloned.1.call-start
  7.2 1.5 copy-done
  8.8 5.7 %fusion.17 = f32[1024,256]{1,0:T(8,128)S(1)} fusion(bf16[1024,4096]{1,0:T(8,128)(2,1)} %param.2, bf16[4096,256]{1,0:T(8,128)(2,1)S(1)} %copy-done), kind=kOutput, calls=%fused_computation.40 | convolution fusion | flops 2147483648 | bytes 11534336 | tf_op jit(solution)/shard_map/dot_general | solution.py:13
  14.5 2.5 fusion.18
  17.0 0.0 all-reduce.5.cloned.1.call-update
  17.0 0.0 all-reduce.7.cloned.1.call-start
  17.1 32.1 %all-reduce.5.cloned.1.call-done = f32[256,256]{0,1:T(8,128)} async-done(((f32[256,256]{0,1:T(8,128)}), f32[256,256]{0,1:T(8,128)}) %all-reduce.5.cloned.1.call-update) | async-done | bytes 262160 | tf_op jit(solution)/shard_map/psum | solution.py:24
  49.2 0.0 all-reduce.7.cloned.1.call-update
  49.2 0.2 all-reduce.9.cloned.1.call-start
  49.4 7.7 %fusion = f32[256,4096]{1,0:T(8,128)} fusion(bf16[1024,4096]{1,0:T(8,128)(2,1)} %param.2, f32[1024,256]{1,0:T(8,128)S(1)} %fusion.17), kind=kOutput, calls=%fused_computation.5 | convolution fusion | flops 2147745792 | bytes 13631488 | tf_op jit(solution)/shard_map/dot_general | solution.py:16
  57.2 0.0 all-reduce.9.cloned.1.call-update
  57.2 0.6 iota_compare_fusion
  57.9 213.8 %all-reduce.7.cloned.1.call-done = f32[256,256]{0,1:T(8,128)} async-done(((f32[256,256]{0,1:T(8,128)}), f32[256,256]{0,1:T(8,128)}) %all-reduce.7.cloned.1.call-update) | async-done | bytes 262160 | tf_op jit(solution)/shard_map/psum | solution.py:24
  271.6 1.1 copy.6
  272.7 1.0 fusion.2
  273.7 0.0 copy-start.2
  273.7 0.7 copy-done.2
  274.4 11.7 %cholesky.50 = f32[128,128]{1,0:T(8,128)S(1)} custom-call(f32[128,128]{1,0:T(8,128)S(1)} %cholesky.118), custom_call_target="Cholesky" | custom-call | tf_op jit(solution)/shard_map/jit(cholesky)/cholesky | solution.py:25
  286.2 9.8 %custom-call.14 = f32[1,128,128]{1,2,0:T(8,128)S(1)} custom-call(f32[1,128,128]{2,1,0:T(8,128)S(1)} %get-tuple-element.29), custom_call_target="InvertDiagBlocksLowerTriangular" | custom-call | tf_op jit(solution)/shard_map/jit(cholesky)/cholesky | solution.py:25
  296.0 1.0 constant_dynamic-update-slice_fusion
  297.0 1.1 convolution_subtract_fusion.1
  298.2 11.9 %cholesky.105 = f32[128,128]{1,0:T(8,128)S(1)} custom-call(f32[128,128]{1,0:T(8,128)S(1)} %convolution_subtract_fusion.1), custom_call_target="Cholesky" | custom-call | tf_op jit(solution)/shard_map/jit(cholesky)/cholesky | solution.py:25
  310.0 0.0 copy-start.1
  310.1 0.6 compare_reduce_fusion
  311.9 0.0 copy-done.1
  311.9 1.7 multiply_bitcast_fusion
  313.6 0.1 triangular_solve.63
  313.7 5.0 while.1
  313.7 0.6 fusion.30
  314.3 1.9 bitcast_dynamic-update-slice_fusion.2
  316.2 0.6 fusion.30
  316.8 1.9 bitcast_dynamic-update-slice_fusion.2
  318.7 21.1 %custom-call.15 = f32[2,128,128]{1,2,0:T(8,128)} custom-call(f32[2,128,128]{2,1,0:T(8,128)} %get-tuple-element.10), custom_call_target="InvertDiagBlocksLowerTriangular" | custom-call | tf_op jit(solution)/shard_map/triangular_solve | solution.py:28
  339.8 1.8 copy.7
  341.6 1.1 fusion.6
  342.7 1.0 convolution_subtract_fusion
  343.7 1.2 fusion.9
  344.9 2.0 convolution_multiply_fusion
  346.9 198.5 %all-reduce.9.cloned.1.call-done = f32[256,4096]{1,0:T(8,128)} async-done(((f32[256,4096]{1,0:T(8,128)}), f32[256,4096]{1,0:T(8,128)}) %all-reduce.9.cloned.1.call-update) | async-done | bytes 4194320 | tf_op jit(solution)/shard_map/psum | solution.py:20
  545.5 1.9 fusion.4
  (8 shorter events, 0.1 us)
Async XLA Ops:
  7.2 1.6 copy-start
  7.2 42.0 %all-reduce.5.cloned.1.call-start = ((), (), s32[]{:S(2)}) async-start(), calls=%async_computation | async-start | bytes 524288 | tf_op jit(solution)/shard_map/psum | solution.py:24
  17.0 254.6 %all-reduce.7.cloned.1.call-start = ((), (), s32[]{:S(2)}) async-start(), calls=%async_computation.1 | async-start | bytes 524288 | tf_op jit(solution)/shard_map/psum | solution.py:24
  49.2 496.2 %all-reduce.9.cloned.1.call-start = ((), (), s32[]{:S(2)}) async-start(), calls=%async_computation.2 | async-start | bytes 8388608 | tf_op jit(solution)/shard_map/psum | solution.py:20
  273.7 0.7 copy-start.2
  310.0 1.9 copy-start.1
Sparse Core Ops, SparseCore 0:
  17.1 31.9 all-reduce.4
  54.6 216.9 all-reduce.6
  277.1 268.3 all-reduce.8

commit v2 on v0

--- a/solution.py
+++ b/solution.py
@@ -18,7 +18,9 @@
     columns = movie.shape[1] // devices_all
     total = lax.psum(partial_sum, ("vox", "sub"))
     mine = lax.dynamic_slice_in_dim(total, lax.axis_index(("vox", "sub")) * columns, columns, 1)
-    gram = lax.psum(square_sum(sketch), ("vox", "sub"))
+    part = square_sum(sketch)
+    parts = lax.all_gather(part, ("vox", "sub"), axis=0, tiled=False)
+    gram = parts.sum(axis=0)
     lower = jnp.linalg.cholesky(gram)
     width = sketch.shape[1]
     identity = jnp.eye(width, dtype=jnp.float32)

time: 381 us -> 515 us (1.35)
  waiting for transfers between devices: 274 us -> 383 us
  other arithmetic: 58.5 us -> 80.1 us
    all_gather x0 -> x1, waiting for transfers between devices: none -> 207 us  [local(): parts = lax.all_gather(part, ('vox', 'sub'), axis=0, tiled=False)]
    psum x1, waiting for transfers between devices: 274 us -> 176 us  [local(): total = lax.psum(partial_sum, ('vox', 'sub'))]
    reduce_sum x0 -> x1, other arithmetic: none -> 21.6 us  [local(): gram = parts.sum(axis=0)]
  transfers between devices with their start and end apart: 1 -> 2, of which waited for: 1 -> 2; matrix products, arithmetic and copies ran while one was open for 0% -> 20% of each run, Pallas kernels for 0% -> 0%
where the time goes in v2:
time: 515 us; the launch traced here: 514 us
  waiting for transfers between devices  383 us (74%)
  other arithmetic  80.1 us (16%)
  matrix products  25.3 us (5%)
  between operations  15.5 us (3%)
  local copies, waits for them, and re-layouts  10.3 us (2%)
    all_gather x1, waiting for transfers between devices, local(): parts = lax.all_gather(part, ('vox', 'sub'), axis=0, tiled=False)  207 us
    psum x1, waiting for transfers between devices, local(): total = lax.psum(partial_sum, ('vox', 'sub'))  176 us
    another operation x6, other arithmetic, local(): lower = jnp.linalg.cholesky(gram)  34 us
    reduce_sum x1, other arithmetic, local(): gram = parts.sum(axis=0)  21.6 us
    another operation x2, other arithmetic, local(): lax.linalg.triangular_solve(lower, identity, left_side=True, lower=True)  21.1 us
  transfers between devices with their start and end apart: 2, of which 2 were waited for; matrix products, arithmetic and copies ran while one was open for 20% of the time, Pallas kernels for 0%

profile of v2, /device:TPU:2, one launch (start us, length us, event | category | flops | bytes accessed | tf_op | source)
XLA Modules:
  0.0 514.2 jit_solution(8533228719686255634)
XLA Ops:
  7.2 0.0 copy-start
  7.2 0.0 all-gather.3.cloned.1.call-start
  7.2 1.5 copy-done
  8.8 5.7 %fusion.17 = f32[1024,256]{1,0:T(8,128)S(1)} fusion(bf16[1024,4096]{1,0:T(8,128)(2,1)} %param.2, bf16[4096,256]{1,0:T(8,128)(2,1)S(1)} %copy-done), kind=kOutput, calls=%fused_computation.40 | convolution fusion | flops 2147483648 | bytes 11534336 | tf_op jit(solution)/shard_map/dot_general | solution.py:12
  14.5 2.5 fusion.18
  17.0 0.0 all-gather.3.cloned.1.call-update
  17.0 0.0 all-reduce.3.cloned.1.call-start
  17.1 7.7 %fusion = f32[256,4096]{1,0:T(8,128)} fusion(bf16[1024,4096]{1,0:T(8,128)(2,1)} %param.2, f32[1024,256]{1,0:T(8,128)S(1)} %fusion.17), kind=kOutput, calls=%fused_computation.5 | convolution fusion | flops 2147745792 | bytes 13631488 | tf_op jit(solution)/shard_map/dot_general | solution.py:15
  24.8 0.0 all-reduce.3.cloned.1.call-update
  24.8 0.6 iota_compare_fusion
  25.5 206.6 %all-gather.3.cloned.1.call-done = f32[65536,256]{1,0:T(8,128)} async-done(((f32[256,256]{1,0:T(8,128)}), f32[65536,256]{1,0:T(8,128)}) %all-gather.3.cloned.1.call-update) | async-done | bytes 67108880 | tf_op jit(solution)/shard_map/all_gather | solution.py:22
  232.1 21.6 %reduce_sum.9 = f32[256,256]{1,0:T(8,128)S(1)} reduce(f32[256,256,256]{2,1,0:T(8,128)} %bitcast, f32[]{:T(128)} %constant.85.clone.1), dimensions={0}, to_apply=%region_0.0 | reduce | flops 16711680 | bytes 67371008 | tf_op jit(solution)/shard_map/reduce_sum | solution.py:23
  253.7 0.8 copy.7
  254.6 1.0 fusion.2
  255.6 0.0 copy-start.2
  255.6 0.7 copy-done.2
  256.3 11.7 %cholesky.50 = f32[128,128]{1,0:T(8,128)S(1)} custom-call(f32[128,128]{1,0:T(8,128)S(1)} %cholesky.118), custom_call_target="Cholesky" | custom-call | tf_op jit(solution)/shard_map/jit(cholesky)/cholesky | solution.py:24
  268.1 9.8 %custom-call.14 = f32[1,128,128]{1,2,0:T(8,128)S(1)} custom-call(f32[1,128,128]{2,1,0:T(8,128)S(1)} %get-tuple-element.32), custom_call_target="InvertDiagBlocksLowerTriangular" | custom-call | tf_op jit(solution)/shard_map/jit(cholesky)/cholesky | solution.py:24
  277.9 1.0 constant_dynamic-update-slice_fusion
  278.9 1.1 convolution_subtract_fusion.1
  280.0 11.7 %cholesky.105 = f32[128,128]{1,0:T(8,128)S(1)} custom-call(f32[128,128]{1,0:T(8,128)S(1)} %convolution_subtract_fusion.1), custom_call_target="Cholesky" | custom-call | tf_op jit(solution)/shard_map/jit(cholesky)/cholesky | solution.py:24
  291.8 0.0 copy-start.1
  291.8 0.7 compare_reduce_fusion
  293.9 0.0 copy-done.1
  293.9 1.7 multiply_bitcast_fusion
  295.6 0.1 triangular_solve.63
  295.6 5.3 %while.1 = (s32[]{:T(128)}, f32[256,256]{1,0:T(8,128)S(1)}, s32[2,2]{1,0:T(2,128)S(1)}, f32[2,128,128]{2,1,0:T(8,128)}, s32[]{:T(128)}) while((s32[]{:T(128)}, f32[256,256]{1,0:T(8,128)S(1)}, s32[2,2]{1,0:T(2,128)S(1)}, f32[2,128,128]{2,1,0:T(8,128)}, s32[]{:T(128)}) %tuple.30), condition=%wide.while_cond, body=%wide.while_body.sunk | while | flops 2 | bytes 132705 | solution.py:27
  295.6 0.6 fusion.30
  296.2 2.0 bitcast_dynamic-update-slice_fusion.2
  298.3 0.6 fusion.30
  298.9 2.0 bitcast_dynamic-update-slice_fusion.2
  300.9 21.1 %custom-call.15 = f32[2,128,128]{1,2,0:T(8,128)} custom-call(f32[2,128,128]{2,1,0:T(8,128)} %get-tuple-element.10), custom_call_target="InvertDiagBlocksLowerTriangular" | custom-call | tf_op jit(solution)/shard_map/triangular_solve | solution.py:27
  322.0 1.8 copy.8
  323.8 1.1 fusion.6
  324.9 1.0 convolution_subtract_fusion
  325.9 1.1 fusion.9
  327.1 2.0 convolution_multiply_fusion
  329.1 176.3 %all-reduce.3.cloned.1.call-done = f32[256,4096]{1,0:T(8,128)} async-done(((f32[256,4096]{1,0:T(8,128)}), f32[256,4096]{1,0:T(8,128)}) %all-reduce.3.cloned.1.call-update) | async-done | bytes 4194320 | tf_op jit(solution)/shard_map/psum | solution.py:19
  505.4 1.9 fusion.4
  (8 shorter events, 0.1 us)
Async XLA Ops:
  7.2 1.6 copy-start
  7.2 224.9 %all-gather.3.cloned.1.call-start = ((), (), s32[]{:S(2)}) async-start(), calls=%async_computation.1 | async-start | bytes 67371008 | tf_op jit(solution)/shard_map/all_gather | solution.py:22
  17.0 488.3 %all-reduce.3.cloned.1.call-start = ((), (), s32[]{:S(2)}) async-start(), calls=%async_computation | async-start | bytes 8388608 | tf_op jit(solution)/shard_map/psum | solution.py:19
  255.6 0.7 copy-start.2
  291.8 2.1 copy-start.1
Sparse Core Ops, SparseCore 0:
  17.2 214.8 all-gather.2
  237.6 267.7 all-reduce.2
